TPU v7x, 256 devices: a whole 4x4x8 slice. The times are simulated.
256 devices in a mesh: shard: 64 (over z, x, core), model: 4 (over y).
Axes of the slice: x: 4, y: 4, z: 8, core: 2. Of those that a mesh axis runs over, the one named last changes fastest.
Arguments:
- grad_stack: float32 [512, 128, 2048], P(None, 'shard', 'model'), may hold values from -6 to 6
- moment_stack: float32 [512, 128, 2048], P(None, 'shard', 'model'), may hold values from -6 to 6
- weight_stack: float32 [512, 128, 2048], P(None, 'shard', 'model'), may hold values from -0.1875 to 0.1875
Outputs:
- new_weights: float32 [512, 128, 2048], P(None, 'shard', 'model')
- new_momentum: float32 [512, 128, 2048], P(None, 'shard', 'model')
All inputs are finite; a program needn't handle non-finite values.
Results may differ from a plain program's by a relative error of at most 0.00021.
Values sent between devices are 32-bit elements; how exact they have to be, the bound alone decides.
A program may use at most 64 MiB of HBM per device.

v0:
```python
import jax
import jax.numpy as jnp
from jax import lax
from jax.sharding import PartitionSpec as P

hold_rate = 0.95
learn_rate = 1.0
decay_rate = 0.1
HIGH = lax.Precision.HIGHEST


def mul(a, b):
    return jnp.einsum("mij,mjk->mik", a, b, precision=HIGH)


def chain(gram, steps):
    eye = jnp.eye(gram.shape[-1], dtype=gram.dtype)
    total = None
    for step in range(steps):
        factor = 3.4445 * eye - 4.775 * gram + 2.0315 * mul(gram, gram)
        total = factor if total is None else mul(factor, total)
        if step < steps - 1:
            gram = mul(mul(factor, gram), factor)
    return total


def summed_gram(rows):
    part = jnp.einsum("mik,mjk->mij", rows, rows, precision=HIGH)
    parts = lax.all_to_all(part, "model", split_axis=0, concat_axis=0, tiled=True)
    return parts.reshape(4, -1, *parts.shape[1:]).sum(axis=0)


def on_device(grad_stack, moment_stack, weight_stack):
    new_momentum = hold_rate * moment_stack + grad_stack
    rows = lax.all_to_all(new_momentum, "shard", split_axis=0, concat_axis=1, tiled=True)
    gram = summed_gram(rows)
    scale = lax.rsqrt(jnp.trace(gram, axis1=1, axis2=2)[:, None, None] + 1e-06)
    first = chain(gram * scale * scale, 2) * scale
    rows = mul(lax.all_gather(first, "model", axis=0, tiled=True), rows)
    second = chain(summed_gram(rows), 3)
    rows = mul(lax.all_gather(second, "model", axis=0, tiled=True), rows)
    back = lax.all_to_all(rows, "shard", split_axis=1, concat_axis=0, tiled=True)
    new_weights = (1.0 - learn_rate * decay_rate) * weight_stack - learn_rate * back
    return (new_weights, new_momentum)


def solution(mesh):
    spec = P(None, "shard", "model")
    return jax.shard_map(
        on_device, mesh=mesh, in_specs=(spec,) * 3, out_specs=(spec,) * 2, check_vma=False
    )
```

profile of v0, /device:TPU:2, one launch (start us, length us, event | category | flops | bytes accessed | tf_op | source)
XLA Modules:
  0.0 198.5 jit_solution(3235271127646908158)
XLA Ops:
  0.6 3.7 %multiply_add_fusion = f32[512,2,512]{2,1,0:T(2,128)S(1)} fusion(f32[512,2,512]{2,1,0:T(2,128)} %param.3, f32[512,2,512]{2,1,0:T(2,128)} %param.4), kind=kLoop, calls=%fused_computation.2 | loop fusion | flops 1048576 | bytes 6291456 | tf_op jit(solution)/shard_map/add | solution.py:34
  4.3 0.0 copy-start.2
  4.3 63.1 %all_to_all.46 = f32[512,2,512]{2,1,0:T(2,128)S(1)} all-to-all(f32[512,2,512]{2,1,0:T(2,128)S(1)} %multiply_add_fusion), channel_id=1, replica_groups=mesh['shard'=64,'model'=4] {'shard'}, dimensions={0} | all-to-all | bytes 4194304 | tf_op jit(solution)/shard_map/all_to_all | solution.py:35
  67.4 0.0 copy-done.2
  67.4 2.1 %copy.11 = f32[64,8,2,512]{3,2,0,1:T(2,128)} copy(f32[64,8,2,512]{3,2,1,0:T(2,128)S(1)} %bitcast.46) | data formatting | bytes 4194304 | tf_op jit(solution)/shard_map/all_to_all | solution.py:35
  69.4 2.7 %all_to_all.35 = f32[8,128,512]{2,1,0:T(8,128)S(1)} reshape(f32[8,64,2,512]{3,2,1,0:T(2,128)} %bitcast.44) | data formatting | bytes 4194304 | tf_op jit(solution)/shard_map/all_to_all | solution.py:35
  72.1 2.9 %fusion.8 = f32[8,128,128]{2,1,0:T(8,128)} fusion(f32[8,128,512]{2,1,0:T(8,128)S(1)} %all_to_all.35), kind=kOutput, calls=%fused_computation.22 | convolution fusion | flops 805306368 | bytes 2621440 | tf_op jit(solution)/shard_map/mik,mjk->mij/dot_general | solution.py:28
  75.0 4.5 %all-to-all-start.1 = ((f32[8,128,128]{2,1,0:T(8,128)}), f32[8,128,128]{2,1,0:T(8,128)S(1)}, u32[]{:S(2)}, u32[]{:S(2)}) async-start(f32[8,128,128]{2,1,0:T(8,128)} %fusion.8), calls=%async_computation.1 | async-start | bytes 1048576 | tf_op jit(solution)/shard_map/all_to_all | solution.py:29
  79.5 8.0 %all-to-all-done.1 = f32[8,128,128]{2,1,0:T(8,128)S(1)} async-done(((f32[8,128,128]{2,1,0:T(8,128)}), f32[8,128,128]{2,1,0:T(8,128)S(1)}, u32[]{:S(2)}, u32[]{:S(2)}) %all-to-all-start.1) | async-done | bytes 524320 | tf_op jit(solution)/shard_map/all_to_all | solution.py:29
  87.6 0.1 select_reduce_fusion
  87.7 0.4 fusion.4
  88.1 0.3 fusion.5
  88.4 0.3 fusion.9
  88.7 0.3 fusion.3
  89.0 0.3 convolution_multiply_fusion.3
  89.2 12.8 %all_gather.6 = f32[8,128,128]{2,1,0:T(8,128)S(1)} all-gather(f32[2,128,128]{2,1,0:T(8,128)S(1)} %convolution_multiply_fusion.3), channel_id=1, replica_groups=mesh['shard'=64,'model'=4] {'model'}, dimensions={0}, use_global_device_ids=true | all-gather | bytes 655360 | tf_op jit(solution)/shard_map/all_gather | solution.py:39
  102.0 1.8 fusion.10
  103.9 0.0 copy-start
  103.9 2.1 %fusion.11 = f32[8,128,128]{2,1,0:T(8,128)S(1)} fusion(f32[8,128,512]{2,1,0:T(8,128)S(1)} %fusion.10), kind=kOutput, calls=%fused_computation.25 | convolution fusion | flops 805306368 | bytes 2621440 | tf_op jit(solution)/shard_map/mik,mjk->mij/dot_general | solution.py:28
  106.0 0.0 copy-done
  106.0 11.3 %all_to_all.47 = f32[8,128,128]{2,1,0:T(8,128)S(1)} all-to-all(f32[8,128,128]{2,1,0:T(8,128)S(1)} %fusion.11), channel_id=1, replica_groups=mesh['shard'=64,'model'=4] {'model'}, dimensions={0} | all-to-all | bytes 1048576 | tf_op jit(solution)/shard_map/all_to_all | solution.py:29
  117.3 0.0 copy-start.1
  117.4 0.3 fusion.2
  117.6 0.3 fusion.12
  117.9 0.3 fusion.13
  118.2 0.3 fusion.1
  118.5 0.3 fusion.16
  118.7 0.3 fusion.14
  119.0 0.3 fusion.15
  119.3 0.3 fusion
  119.6 0.3 fusion.17
  119.8 12.8 %all_gather.7 = f32[8,128,128]{2,1,0:T(8,128)S(1)} all-gather(f32[2,128,128]{2,1,0:T(8,128)S(1)} %fusion.17), channel_id=1, replica_groups=mesh['shard'=64,'model'=4] {'model'}, dimensions={0}, use_global_device_ids=true | all-gather | bytes 655360 | tf_op jit(solution)/shard_map/all_gather | solution.py:41
  132.6 0.0 copy-done.1
  132.6 1.8 fusion.18
  134.5 1.2 copy.8
  135.7 57.6 %all_to_all.48 = f32[8,128,512]{2,0,1:T(8,128)S(1)} all-to-all(f32[8,128,512]{2,0,1:T(8,128)S(1)} %copy.8), channel_id=1, replica_groups=mesh['shard'=64,'model'=4] {'shard'}, dimensions={1} | all-to-all | bytes 4194304 | tf_op jit(solution)/shard_map/all_to_all | solution.py:42
  193.3 0.0 copy-start.3
  193.3 1.9 copy.9
  195.3 0.0 copy-done.3
  195.3 3.3 %bitcast_subtract_fusion = f32[512,2,512]{2,1,0:T(2,128)} fusion(f32[64,8,2,512]{3,2,1,0:T(2,128)S(1)} %copy.9, f32[512,2,512]{2,1,0:T(2,128)S(1)} %copy-done.3), kind=kLoop, calls=%fused_computation | loop fusion | flops 1048576 | bytes 6291456 | tf_op jit(solution)/shard_map/sub | solution.py:43
  (5 shorter events, 0.1 us)
Async XLA Ops:
  4.3 63.1 %copy-start.2 = (f32[512,2,512]{2,1,0:T(2,128)}, f32[512,2,512]{2,1,0:T(2,128)S(1)}, u32[]{:S(2)}) copy-start(f32[512,2,512]{2,1,0:T(2,128)S(1)} %multiply_add_fusion) | copy-start | bytes 6291460
  75.0 12.5 %all-to-all-start.1 = ((f32[8,128,128]{2,1,0:T(8,128)}), f32[8,128,128]{2,1,0:T(8,128)S(1)}, u32[]{:S(2)}, u32[]{:S(2)}) async-start(f32[8,128,128]{2,1,0:T(8,128)} %fusion.8), calls=%async_computation.1 | async-start | bytes 1048576 | tf_op jit(solution)/shard_map/all_to_all | solution.py:29
  103.9 2.1 %copy-start = (f32[8,128,512]{2,1,0:T(8,128)}, f32[8,128,512]{2,1,0:T(8,128)S(1)}, u32[]{:S(2)}) copy-start(f32[8,128,512]{2,1,0:T(8,128)S(1)} %fusion.10) | copy-start | bytes 6291460
  117.3 15.3 %copy-start.1 = (f32[8,128,512]{2,1,0:T(8,128)S(1)}, f32[8,128,512]{2,1,0:T(8,128)}, u32[]{:S(2)}) copy-start(f32[8,128,512]{2,1,0:T(8,128)} %copy-done) | copy-start | bytes 6291460
  193.3 1.9 copy-start.3
where the time goes:
time: 199 us
  blocking collectives  158 us (79%)
  matrix products  12.5 us (6%)
  waiting for transfers between devices  8.05 us (4%)
  local copies, waits for them, and re-layouts  7.95 us (4%)
  other arithmetic  7.12 us (4%)
  starting transfers between devices  4.46 us (2%)
    all_to_all x1, blocking collectives, on_device(): lax.all_to_all(new_momentum, 'shard', split_axis=0, concat_axis=1, tiled=...  63.1 us
    all_to_all x1, blocking collectives, on_device(): lax.all_to_all(rows, 'shard', split_axis=1, concat_axis=0, tiled=True)  57.6 us
    all_gather x1, blocking collectives, on_device(): rows = mul(lax.all_gather(first, 'model', axis=0, tiled=True), rows)  12.8 us
    all_gather x1, blocking collectives, on_device(): rows = mul(lax.all_gather(second, 'model', axis=0, tiled=True), rows)  12.8 us
    all_to_all x1, blocking collectives, summed_gram(): lax.all_to_all(part, 'model', split_axis=0, concat_axis=0, tiled=True)  11.3 us
    all_to_all x1, waiting for transfers between devices, summed_gram(): lax.all_to_all(part, 'model', split_axis=0, concat_axis=0, tiled=True)  8.05 us
    dot_general x16, matrix products, mul(): return jnp.einsum('mij,mjk->mik', a, b, precision=HIGH)  7.6 us
    dot_general x2, matrix products, summed_gram(): part = jnp.einsum('mik,mjk->mij', rows, rows, precision=HIGH)  4.93 us
  transfers between devices with their start and end apart: 1, of which 1 were waited for; matrix products, arithmetic and copies ran while one was open for 0% of the time, Pallas kernels for 0%

commit v1 on v0

--- a/solution.py
+++ b/solution.py
@@ -39,7 +39,9 @@
     rows = mul(lax.all_gather(first, "model", axis=0, tiled=True), rows)
     second = chain(summed_gram(rows), 3)
     rows = mul(lax.all_gather(second, "model", axis=0, tiled=True), rows)
-    back = lax.all_to_all(rows, "shard", split_axis=1, concat_axis=0, tiled=True)
+    pieces = jnp.split(rows, lax.axis_size("shard"), axis=1)
+    received = lax.all_to_all(jnp.stack(pieces), "shard", 0, 0)
+    back = jnp.concatenate(received, axis=0)
     new_weights = (1.0 - learn_rate * decay_rate) * weight_stack - learn_rate * back
     return (new_weights, new_momentum)
 

time: 199 us -> 198 us (level)
  no operation moved by 1% of the time
where the time goes in v1:
time: 198 us; the launch traced here: 197 us
  blocking collectives  158 us (80%)
  matrix products  12.5 us (6%)
  waiting for transfers between devices  8.05 us (4%)
  other arithmetic  7.12 us (4%)
  local copies, waits for them, and re-layouts  6.18 us (3%)
  starting transfers between devices  4.46 us (2%)
    all_to_all x1, blocking collectives, on_device(): lax.all_to_all(new_momentum, 'shard', split_axis=0, concat_axis=1, tiled=...  63.1 us
    all_to_all x1, blocking collectives, on_device(): received = lax.all_to_all(jnp.stack(pieces), 'shard', 0, 0)  57.8 us
    all_gather x1, blocking collectives, on_device(): rows = mul(lax.all_gather(first, 'model', axis=0, tiled=True), rows)  12.8 us
    all_gather x1, blocking collectives, on_device(): rows = mul(lax.all_gather(second, 'model', axis=0, tiled=True), rows)  12.8 us
    all_to_all x1, blocking collectives, summed_gram(): lax.all_to_all(part, 'model', split_axis=0, concat_axis=0, tiled=True)  11.3 us
    all_to_all x1, waiting for transfers between devices, summed_gram(): lax.all_to_all(part, 'model', split_axis=0, concat_axis=0, tiled=True)  8.05 us
    dot_general x16, matrix products, mul(): return jnp.einsum('mij,mjk->mik', a, b, precision=HIGH)  7.6 us
    dot_general x2, matrix products, summed_gram(): part = jnp.einsum('mik,mjk->mij', rows, rows, precision=HIGH)  4.93 us
  transfers between devices with their start and end apart: 1, of which 1 were waited for; matrix products, arithmetic and copies ran while one was open for 0% of the time, Pallas kernels for 0%

profile of v1, /device:TPU:2, one launch (start us, length us, event | category | flops | bytes accessed | tf_op | source)
XLA Modules:
  0.0 197.3 jit_solution(1204164117297704647)
XLA Ops:
  0.6 3.7 %multiply_add_fusion = f32[512,2,512]{2,1,0:T(2,128)S(1)} fusion(f32[512,2,512]{2,1,0:T(2,128)} %param.3, f32[512,2,512]{2,1,0:T(2,128)} %param.4), kind=kLoop, calls=%fused_computation.2 | loop fusion | flops 1048576 | bytes 6291456 | tf_op jit(solution)/shard_map/add | solution.py:34
  4.3 0.0 copy-start.2
  4.3 63.1 %all_to_all.33 = f32[512,2,512]{2,1,0:T(2,128)S(1)} all-to-all(f32[512,2,512]{2,1,0:T(2,128)S(1)} %multiply_add_fusion), channel_id=1, replica_groups=mesh['shard'=64,'model'=4] {'shard'}, dimensions={0} | all-to-all | bytes 4194304 | tf_op jit(solution)/shard_map/all_to_all | solution.py:35
  67.4 0.0 copy-done.2
  67.4 2.1 %copy.8 = f32[64,8,2,512]{3,2,0,1:T(2,128)} copy(f32[64,8,2,512]{3,2,1,0:T(2,128)S(1)} %bitcast.298) | data formatting | bytes 4194304 | tf_op jit(solution)/shard_map/all_to_all | solution.py:35
  69.4 2.7 %all_to_all.25 = f32[8,128,512]{2,1,0:T(8,128)S(1)} reshape(f32[8,64,2,512]{3,2,1,0:T(2,128)} %bitcast.297) | data formatting | bytes 4194304 | tf_op jit(solution)/shard_map/all_to_all | solution.py:35
  72.1 2.9 %fusion.8 = f32[8,128,128]{2,1,0:T(8,128)} fusion(f32[8,128,512]{2,1,0:T(8,128)S(1)} %all_to_all.25), kind=kOutput, calls=%fused_computation.150 | convolution fusion | flops 805306368 | bytes 2621440 | tf_op jit(solution)/shard_map/mik,mjk->mij/dot_general | solution.py:28
  75.0 4.5 %all-to-all-start.1 = ((f32[8,128,128]{2,1,0:T(8,128)}), f32[8,128,128]{2,1,0:T(8,128)S(1)}, u32[]{:S(2)}, u32[]{:S(2)}) async-start(f32[8,128,128]{2,1,0:T(8,128)} %fusion.8), calls=%async_computation.1 | async-start | bytes 1048576 | tf_op jit(solution)/shard_map/all_to_all | solution.py:29
  79.5 8.0 %all-to-all-done.1 = f32[8,128,128]{2,1,0:T(8,128)S(1)} async-done(((f32[8,128,128]{2,1,0:T(8,128)}), f32[8,128,128]{2,1,0:T(8,128)S(1)}, u32[]{:S(2)}, u32[]{:S(2)}) %all-to-all-start.1) | async-done | bytes 524320 | tf_op jit(solution)/shard_map/all_to_all | solution.py:29
  87.6 0.1 select_reduce_fusion
  87.7 0.4 fusion.4
  88.1 0.3 fusion.5
  88.4 0.3 fusion.9
  88.7 0.3 fusion.3
  89.0 0.3 convolution_multiply_fusion.3
  89.2 12.8 %all_gather.6 = f32[8,128,128]{2,1,0:T(8,128)S(1)} all-gather(f32[2,128,128]{2,1,0:T(8,128)S(1)} %convolution_multiply_fusion.3), channel_id=1, replica_groups=mesh['shard'=64,'model'=4] {'model'}, dimensions={0}, use_global_device_ids=true | all-gather | bytes 655360 | tf_op jit(solution)/shard_map/all_gather | solution.py:39
  102.0 1.8 fusion.10
  103.9 0.0 copy-start
  103.9 2.1 %fusion.11 = f32[8,128,128]{2,1,0:T(8,128)S(1)} fusion(f32[8,128,512]{2,1,0:T(8,128)S(1)} %fusion.10), kind=kOutput, calls=%fused_computation.153 | convolution fusion | flops 805306368 | bytes 2621440 | tf_op jit(solution)/shard_map/mik,mjk->mij/dot_general | solution.py:28
  106.0 0.0 copy-done
  106.0 11.3 %all_to_all.34 = f32[8,128,128]{2,1,0:T(8,128)S(1)} all-to-all(f32[8,128,128]{2,1,0:T(8,128)S(1)} %fusion.11), channel_id=1, replica_groups=mesh['shard'=64,'model'=4] {'model'}, dimensions={0} | all-to-all | bytes 1048576 | tf_op jit(solution)/shard_map/all_to_all | solution.py:29
  117.3 0.0 copy-start.1
  117.4 0.3 fusion.2
  117.6 0.3 fusion.12
  117.9 0.3 fusion.13
  118.2 0.3 fusion.1
  118.5 0.3 fusion.16
  118.7 0.3 fusion.14
  119.0 0.3 fusion.15
  119.3 0.3 fusion
  119.6 0.3 fusion.17
  119.8 12.8 %all_gather.7 = f32[8,128,128]{2,1,0:T(8,128)S(1)} all-gather(f32[2,128,128]{2,1,0:T(8,128)S(1)} %fusion.17), channel_id=1, replica_groups=mesh['shard'=64,'model'=4] {'model'}, dimensions={0}, use_global_device_ids=true | all-gather | bytes 655360 | tf_op jit(solution)/shard_map/all_gather | solution.py:41
  132.6 0.0 copy-done.1
  132.6 1.8 fusion.18
  136.2 0.0 copy-start.3
  136.2 57.8 %all_to_all.35 = f32[64,8,2,512]{3,2,1,0:T(2,128)S(1)} all-to-all(f32[64,8,2,512]{3,2,1,0:T(2,128)S(1)} %constant_dynamic-update-slice_fusion), channel_id=1, replica_groups=mesh['shard'=64,'model'=4] {'shard'}, dimensions={0} | all-to-all | bytes 4194304 | tf_op jit(solution)/shard_map/all_to_all | solution.py:43
  194.0 0.0 copy-done.3
  194.0 3.3 %bitcast_subtract_fusion = f32[512,2,512]{2,1,0:T(2,128)} fusion(f32[64,8,2,512]{3,2,1,0:T(2,128)S(1)} %all_to_all.35, f32[512,2,512]{2,1,0:T(2,128)S(1)} %copy-done.3), kind=kLoop, calls=%fused_computation | loop fusion | flops 1048576 | bytes 6291456 | tf_op jit(solution)/shard_map/sub | solution.py:45
  (69 shorter events, 1.5 us)
Async XLA Ops:
  4.3 63.1 %copy-start.2 = (f32[512,2,512]{2,1,0:T(2,128)}, f32[512,2,512]{2,1,0:T(2,128)S(1)}, u32[]{:S(2)}) copy-start(f32[512,2,512]{2,1,0:T(2,128)S(1)} %multiply_add_fusion) | copy-start | bytes 6291460
  75.0 12.5 %all-to-all-start.1 = ((f32[8,128,128]{2,1,0:T(8,128)}), f32[8,128,128]{2,1,0:T(8,128)S(1)}, u32[]{:S(2)}, u32[]{:S(2)}) async-start(f32[8,128,128]{2,1,0:T(8,128)} %fusion.8), calls=%async_computation.1 | async-start | bytes 1048576 | tf_op jit(solution)/shard_map/all_to_all | solution.py:29
  103.9 2.1 %copy-start = (f32[8,128,512]{2,1,0:T(8,128)}, f32[8,128,512]{2,1,0:T(8,128)S(1)}, u32[]{:S(2)}) copy-start(f32[8,128,512]{2,1,0:T(8,128)S(1)} %fusion.10) | copy-start | bytes 6291460
  117.3 15.3 %copy-start.1 = (f32[8,128,512]{2,1,0:T(8,128)S(1)}, f32[8,128,512]{2,1,0:T(8,128)}, u32[]{:S(2)}) copy-start(f32[8,128,512]{2,1,0:T(8,128)} %copy-done) | copy-start | bytes 6291460
  136.2 57.8 %copy-start.3 = (f32[512,2,512]{2,1,0:T(2,128)S(1)}, f32[512,2,512]{2,1,0:T(2,128)}, u32[]{:S(2)}) copy-start(f32[512,2,512]{2,1,0:T(2,128)} %param.5) | copy-start | bytes 6291460
